TPU v7x, 16 devices: a whole 2x2x2 slice. The times are simulated.
16 devices in a mesh: col: 4 (over z, y), row: 4 (over x, core).
Axes of the slice: x: 2, y: 2, z: 2, core: 2. Of those that a mesh axis runs over, the one named last changes fastest.
Arguments:
- forcing: float32 [2, 192, 192, 256], P(None, 'row', 'col')
- init_guess: float32 [2, 192, 192, 256], P(None, 'row', 'col')
- cell_coef: float32 [2, 192, 192], P(None, 'row', 'col')
- solve_rows: bfloat16 [2, 4, 4, 2304, 3136], P(None, 'row', 'col')
- relax_factor: float32 [2], replicated
Outputs:
- output: float32 [2, 192, 192, 256], P(None, 'row', 'col')
All inputs are finite; a program needn't handle non-finite values.
Results may differ from a plain program's by a relative error of at most 0.00114.
Values are sent between devices in bfloat16 or wider.
A program may use at most 1 GiB of HBM per device.

v0:
```python
import jax
import jax.numpy as jnp
from jax import lax
from jax.experimental import pallas as pl
from jax.experimental.pallas import tpu as pltpu
from jax.sharding import PartitionSpec as P

SWEEPS = 4
MESH_ID = pl.DeviceIdType.MESH
NB = 48
MG = 4
EX = NB + 2 * MG
LANES = 128
CHUNKS = 3
S_COPIES = 4
SIDES = ((-1, 0), (1, 0), (0, -1), (0, 1))
OPP_SIDE = (1, 0, 3, 2)
CORNERS = ((-1, -1), (-1, 1), (1, -1), (1, 1))
F32 = jnp.float32
BF16 = jnp.bfloat16


def kernel(f_hbm, u_hbm, c_ref, s_hbm, om_ref, out_hbm,
           S, Z, R, W, U, C, FX, FY, FE, ces, cer, zes, zer, frs, frr, crs, crr,
           sem_f, sem_u, sem_s, sem_o, sem_cs, sem_cr, sem_zs, sem_zr,
           sem_fs, sem_fr, sem_ks, sem_kr):
    row = lax.axis_index("row")
    col = lax.axis_index("col")
    has_side = (row > 0, row < 3, col > 0, col < 3)
    has_corner = tuple(
        jnp.logical_and(has_side[0] if dr < 0 else has_side[1], has_side[2] if dc < 0 else has_side[3])
        for dr, dc in CORNERS)

    def dev(delta):
        return {"row": row + delta[0], "col": col + delta[1]}

    def ext_col(j):
        return pl.ds(EX * MG + j, NB, stride=EX)

    def own_row(i):
        return pl.ds(EX * (MG + i) + MG, NB)

    def u_copy(s, h):
        return pltpu.make_async_copy(u_hbm.at[s, :, :, pl.ds(h * LANES, LANES)], Z.at[s, h, pl.ds(1, NB), pl.ds(8, NB), :], sem_u.at[s, h])

    def f_copy(s, h):
        return pltpu.make_async_copy(f_hbm.at[s, :, :, pl.ds(h * LANES, LANES)], U.at[s, h], sem_f.at[s, h])

    rows_per = NB * NB // CHUNKS
    k_per = EX * EX // S_COPIES

    def s_copy(s, m):
        return pltpu.make_async_copy(s_hbm.at[s, pl.ds(m * k_per, k_per), :], S.at[s, pl.ds(m * k_per, k_per), :], sem_s.at[s, m])

    def o_copy(s, h, m):
        g = NB // CHUNKS
        return pltpu.make_async_copy(U.at[s, h, pl.ds(m * g, g)], out_hbm.at[s, pl.ds(m * g, g), :, pl.ds(h * LANES, LANES)], sem_o.at[s, h, m])

    for s in range(2):
        for h in range(2):
            u_copy(s, h).start()
    for s in range(2):
        for h in range(2):
            f_copy(s, h).start()
    for s in range(2):
        for m in range(S_COPIES):
            s_copy(s, m).start()

    barrier = pltpu.get_barrier_semaphore()
    n_side = sum(h.astype(jnp.int32) for h in has_side) + sum(h.astype(jnp.int32) for h in has_corner)
    for cond, delta in zip(has_side + has_corner, SIDES + CORNERS):
        @pl.when(cond)
        def _(delta=delta):
            pl.semaphore_signal(barrier, inc=1, device_id=dev(delta), device_id_type=MESH_ID)

    for s in range(2):
        c_t = c_ref[s].T
        for i in range(NB):
            C[s, i, 8:EX, :] = jnp.broadcast_to(c_t[:, i:i + 1], (NB, LANES))

    zero_row = jnp.zeros((64, LANES), F32)

    def zero_z(s, h):
        Z[s, h, 0, :, :] = zero_row
        Z[s, h, 49, :, :] = zero_row

        @pl.loop(1, 49)
        def _(i):
            Z[s, h, i, 0:8, :] = jnp.zeros((8, LANES), F32)
            Z[s, h, i, EX:64, :] = jnp.zeros((8, LANES), F32)

    for s in range(2):
        for h in range(2):
            zero_z(s, h)

    @pl.loop(0, 57)
    def _(i):
        for s in range(2):
            for h in range(2):
                R[s, h, pl.ds(pl.multiple_of(EX * i, 8), EX), :] = jnp.zeros((EX, LANES), F32)

    for s in range(2):
        ces[0, s] = C[s, 0, 8:EX, :]
        ces[1, s] = C[s, NB - 1, 8:EX, :]
        ces[2, s] = C[s, :, 8, :]
        ces[3, s] = C[s, :, EX - 1, :]

    pl.semaphore_wait(barrier, n_side)

    def c_send(d):
        return pltpu.make_async_remote_copy(ces.at[d], cer.at[OPP_SIDE[d]], sem_cs.at[d], sem_cr.at[OPP_SIDE[d]], device_id=dev(SIDES[d]), device_id_type=MESH_ID)

    def c_recv(d):
        return pltpu.make_async_remote_copy(ces.at[OPP_SIDE[d]], cer.at[d], sem_cs.at[OPP_SIDE[d]], sem_cr.at[d], device_id=dev(SIDES[d]), device_id_type=MESH_ID)

    for d in range(4):
        @pl.when(has_side[d])
        def _(d=d):
            c_send(d).start()

    def z_send(s, d):
        return pltpu.make_async_remote_copy(zes.at[s, d], zer.at[s, OPP_SIDE[d]], sem_zs.at[s, d], sem_zr.at[s, OPP_SIDE[d]], device_id=dev(SIDES[d]), device_id_type=MESH_ID)

    def z_recv(s, d):
        return pltpu.make_async_remote_copy(zes.at[s, OPP_SIDE[d]], zer.at[s, d], sem_zs.at[s, OPP_SIDE[d]], sem_zr.at[s, d], device_id=dev(SIDES[d]), device_id_type=MESH_ID)

    def f_send(s, d):
        return pltpu.make_async_remote_copy(frs.at[s, d], frr.at[s, OPP_SIDE[d]], sem_fs.at[s, d], sem_fr.at[s, OPP_SIDE[d]], device_id=dev(SIDES[d]), device_id_type=MESH_ID)

    def f_recv(s, d):
        return pltpu.make_async_remote_copy(frs.at[s, OPP_SIDE[d]], frr.at[s, d], sem_fs.at[s, OPP_SIDE[d]], sem_fr.at[s, d], device_id=dev(SIDES[d]), device_id_type=MESH_ID)

    def k_send(s, q, p):
        return pltpu.make_async_remote_copy(crs.at[s, q], crr.at[p, s, 3 - q], sem_ks.at[s, q], sem_kr.at[p, s, 3 - q], device_id=dev(CORNERS[q]), device_id_type=MESH_ID)

    def k_recv(s, q, p):
        return pltpu.make_async_remote_copy(crs.at[s, 3 - q], crr.at[p, s, q], sem_ks.at[s, 3 - q], sem_kr.at[p, s, q], device_id=dev(CORNERS[q]), device_id_type=MESH_ID)

    def when_all(conds, body):
        for i, c in enumerate(conds):
            @pl.when(c)
            def _(i=i):
                body(i)

    def send_z_edges(s):
        for h in range(2):
            zes[s, 2, h] = Z[s, h, 1:NB + 1, 8, :]
            zes[s, 3, h] = Z[s, h, 1:NB + 1, EX - 1, :]
        for h in range(2):
            zes[s, 0, h] = Z[s, h, 1, 8:EX, :]
            zes[s, 1, h] = Z[s, h, NB, 8:EX, :]
        for d in (2, 3, 0, 1):
            @pl.when(has_side[d])
            def _(d=d):
                z_send(s, d).start()

    def stencil(s, om, first):
        @pl.loop(0, NB)
        def _(i):
            ax0 = FX[s, i, :, :]
            ax1 = FX[s, i + 1, :, :]
            ay0 = FY[s, i, 0:NB, :]
            ay1 = FY[s, i, 1:NB + 1, :]
            for h in range(2):
                zc = Z[s, h, i + 1, 8:EX, :]
                zl = Z[s, h, i + 1, 7:EX - 1, :]
                zr = Z[s, h, i + 1, 9:EX + 1, :]
                zu = Z[s, h, i, 8:EX, :]
                zd = Z[s, h, i + 2, 8:EX, :]
                av = ax0 * (zc - zu) - ax1 * (zd - zc) + ay0 * (zc - zl) - ay1 * (zr - zc)
                if first:
                    R[s, h, own_row(i), :] = U[s, h, i] - av
                    U[s, h, i] = zc
                else:
                    R[s, h, own_row(i), :] = R[s, h, own_row(i), :] - om * av
                    U[s, h, i] = U[s, h, i] + om * zc

    def edge_fix(s, om):
        def fix(d):
            z_recv(s, d).wait_recv()
            for h in range(2):
                cells = (own_row(0), own_row(NB - 1), ext_col(MG), ext_col(MG + NB - 1))[d]
                R[s, h, cells, :] = R[s, h, cells, :] + om * (FE[s, d] * zer[s, d, h])
        for d in (0, 1, 2, 3):
            @pl.when(has_side[d])
            def _(d=d):
                fix(d)

    def send_frames(s, p):
        for h in range(2):
            lanes = pl.ds(h * LANES, LANES)
            for a in range(MG):
                frs[s, 2, a, :, lanes] = R[s, h, ext_col(MG + a), :].astype(BF16)
                frs[s, 3, a, :, lanes] = R[s, h, ext_col(NB + a), :].astype(BF16)
                frs[s, 0, a, :, lanes] = R[s, h, own_row(a), :].astype(BF16)
                frs[s, 1, a, :, lanes] = R[s, h, own_row(NB - MG + a), :].astype(BF16)
            for q, (dr, dc) in enumerate(CORNERS):
                r0 = MG if dr < 0 else NB
                c0 = 0 if dc < 0 else NB
                tile = [R[s, h, pl.ds(EX * (r0 + a) + c0, 8), :] for a in range(MG)]
                crs[s, q, :, lanes] = jnp.concatenate(tile, axis=0).astype(BF16)
        for d in (2, 3, 0, 1):
            @pl.when(has_side[d])
            def _(d=d):
                f_send(s, d).start()
        when_all(has_corner, lambda q: k_send(s, q, p).start())

    def recv_frames(s, p):
        def side(d):
            f_recv(s, d).wait_recv()
            for h in range(2):
                lanes = pl.ds(h * LANES, LANES)
                for a in range(MG):
                    v = frr[s, d, a, :, lanes].astype(F32)
                    cells = (own_row(a - MG), own_row(NB + a), ext_col(a), ext_col(MG + NB + a))[d]
                    R[s, h, cells, :] = v

        def corner(q):
            k_recv(s, q, p).wait_recv()
            dr, dc = CORNERS[q]
            r0 = 0 if dr < 0 else MG + NB
            for h in range(2):
                v = crr[p, s, q, :, pl.ds(h * LANES, LANES)].astype(F32)
                for a in range(MG):
                    if dc < 0:
                        R[s, h, pl.ds(EX * (r0 + a), 4), :] = v[8 * a:8 * a + 4]
                    else:
                        R[s, h, pl.ds(EX * (r0 + a) + MG + NB, 4), :] = v[8 * a + 4:8 * a + 8]
        when_all(has_side, side)
        when_all(has_corner, corner)

    def wait_frame_sends(s, p):
        when_all(has_side, lambda d: z_send(s, d).wait_send())
        when_all(has_side, lambda d: f_send(s, d).wait_send())
        when_all(has_corner, lambda q: k_send(s, q, p).wait_send())

    def fill_window(s):
        @pl.loop(0, EX // 2)
        def _(t):
            for h in range(2):
                v = R[s, h, pl.ds(pl.multiple_of(2 * EX * t, 16), 2 * EX), :]
                W[s, pl.ds(pl.multiple_of(2 * EX * t, 16), 2 * EX), pl.ds(h * LANES, LANES)] = v.astype(BF16)

    g = NB // CHUNKS

    def matmul(s, m):
        z = lax.dot_general(S[s, :, pl.ds(m * rows_per, rows_per)], W[s], (((0,), (0,)), ((), ())), preferred_element_type=F32)
        return z.reshape(g, NB, 2 * LANES)

    def matmul_to_z(s):
        for m in range(CHUNKS):
            z = matmul(s, m)
            for h in range(2):
                Z[s, h, pl.ds(1 + m * g, g), 8:EX, :] = z[:, :, h * LANES:(h + 1) * LANES]

    for s in range(2):
        for h in range(2):
            u_copy(s, h).wait()
        send_z_edges(s)
    for s in range(2):
        @pl.loop(1, NB)
        def _(i):
            FX[s, i, :, :] = 0.5 * (C[s, i - 1, 8:EX, :] + C[s, i, 8:EX, :])
        C[s, :, 0:8, :] = jnp.zeros((NB, 8, LANES), F32)

        @pl.loop(0, NB)
        def _(i):
            FY[s, i, 0:NB, :] = 0.5 * (C[s, i, 7:EX - 1, :] + C[s, i, 8:EX, :])
    when_all(has_side, lambda d: c_recv(d).wait_recv())
    for s in range(2):
        for d in range(4):
            own = ces[d, s]
            face = jnp.where(has_side[d], 0.5 * (own + cer[d, s]), own)
            if d == 0:
                FX[s, 0, :, :] = face
            elif d == 1:
                FX[s, NB, :, :] = face
            elif d == 2:
                FY[s, :, 0, :] = face
            else:
                FY[s, :, NB, :] = face
            FE[s, d] = face
    for s in range(2):
        for h in range(2):
            f_copy(s, h).wait()
        stencil(s, None, True)
        edge_fix(s, 1.0)
        send_frames(s, 0)

    for s in range(2):
        for m in range(S_COPIES):
            s_copy(s, m).wait()

    @pl.loop(0, SWEEPS - 1)
    def _(k):
        p = lax.rem(k, 2)
        for s in range(2):
            recv_frames(s, p)
            wait_frame_sends(s, p)
            fill_window(s)
            matmul_to_z(s)
            send_z_edges(s)
        for s in range(2):
            om = om_ref[s]
            stencil(s, om, False)
            edge_fix(s, om)
            send_frames(s, 1 - p)

    last = (SWEEPS - 1) % 2
    for s in range(2):
        recv_frames(s, last)
        wait_frame_sends(s, last)
        fill_window(s)
        for m in range(CHUNKS):
            z = matmul(s, m)
            for h in range(2):
                U[s, h, pl.ds(m * g, g)] = U[s, h, pl.ds(m * g, g)] + om_ref[s] * z[:, :, h * LANES:(h + 1) * LANES]
                o_copy(s, h, m).start()
    when_all(has_side, lambda d: c_send(d).wait_send())
    for s in range(2):
        for h in range(2):
            for m in range(CHUNKS):
                o_copy(s, h, m).wait()


def solution(mesh):
    grid_spec = P(None, "row", "col", None)

    def local(forcing, init_guess, cell_coef, solve_rows, relax_factor):
        num_sys, nb, _, rhs = forcing.shape
        s_mat = jnp.swapaxes(solve_rows, 3, 4).reshape(num_sys, solve_rows.shape[-1], nb * nb)
        any_spec = pl.BlockSpec(memory_space=pl.ANY)
        dma = pltpu.SemaphoreType.DMA
        return pl.pallas_call(
            kernel,
            name="schwarz",
            out_shape=jax.ShapeDtypeStruct(forcing.shape, F32),
            in_specs=[any_spec, any_spec, pl.BlockSpec(memory_space=pltpu.VMEM), any_spec, pl.BlockSpec(memory_space=pltpu.SMEM)],
            out_specs=any_spec,
            scratch_shapes=[
                pltpu.VMEM((2, EX * EX, NB * NB), BF16),
                pltpu.VMEM((2, 2, 50, 64, LANES), F32),
                pltpu.VMEM((2, 2, 57 * EX, LANES), F32),
                pltpu.VMEM((2, EX * EX, 2 * LANES), BF16),
                pltpu.VMEM((2, 2, NB, NB, LANES), F32),
                pltpu.VMEM((2, NB, EX, LANES), F32),
                pltpu.VMEM((2, NB + 1, NB, LANES), F32),
                pltpu.VMEM((2, NB, EX, LANES), F32),
                pltpu.VMEM((2, 4, NB, LANES), F32),
                pltpu.VMEM((4, 2, NB, LANES), F32),
                pltpu.VMEM((4, 2, NB, LANES), F32),
                pltpu.VMEM((2, 4, 2, NB, LANES), F32),
                pltpu.VMEM((2, 4, 2, NB, LANES), F32),
                pltpu.VMEM((2, 4, MG, NB, 2 * LANES), BF16),
                pltpu.VMEM((2, 4, MG, NB, 2 * LANES), BF16),
                pltpu.VMEM((2, 4, 32, 2 * LANES), BF16),
                pltpu.VMEM((2, 2, 4, 32, 2 * LANES), BF16),
                dma((2, 2)), dma((2, 2)), dma((2, S_COPIES)), dma((2, 2, CHUNKS)),
                dma((4,)), dma((4,)), dma((2, 4)), dma((2, 4)),
                dma((2, 4)), dma((2, 4)), dma((2, 4)), dma((2, 2, 4)),
            ],
            compiler_params=pltpu.CompilerParams(collective_id=0, has_side_effects=True, vmem_limit_bytes=66_000_000),
            cost_estimate=pl.CostEstimate(flops=30_000_000_000, bytes_accessed=43_000_000, transcendentals=0),
        )(forcing, init_guess, cell_coef, s_mat, relax_factor)

    return jax.shard_map(local, mesh=mesh, in_specs=(grid_spec, grid_spec, P(None, "row", "col"), P(None, "row", "col", None, None), P(None)), out_specs=grid_spec, check_vma=False)
```

profile of v0, /device:TPU:0, one launch (start us, length us, event | category | flops | bytes accessed | tf_op | source)
XLA Modules:
  0.0 103.6 jit_solution(15559051736822578766)
XLA Ops:
  0.0 98.7 %schwarz.1 = f32[2,48,48,256]{3,2,1,0:T(8,128)} custom-call(f32[2,48,48,256]{3,2,1,0:T(8,128)} %f_hbm.1, f32[2,48,48,256]{3,2,1,0:T(8,128)} %u_hbm.1, f32[2,48,48]{2,1,0:T(8,128)} %c_ref.1, bf16[2,3136,2304]{2,1,0:T(8,128)(2,1)} %bitcast.5, f32[2]{0:T(128)} %om_ref.1), custom_call_target="tpu_custom_call" | custom-call | flops 30000001024 | bytes 43000000 | tf_op jit(solution)/shard_map/schwarz/pallas_call | solution.py:334
  98.7 4.9 %copy.8 = f32[2,48,48,256]{3,2,1,0:T(8,128)} copy(f32[2,48,48,256]{3,2,1,0:T(8,128)} %schwarz.1) | data formatting | bytes 9437184
where the time goes:
time: 104 us
  Pallas kernels  98.7 us (95%)
  local copies, waits for them, and re-layouts  4.86 us (5%)
    pallas_call x1, Pallas kernels, local(): pl.pallas_call(kernel, name='schwarz', out_shape=jax.ShapeDtypeStruct(for...  98.7 us
    unnamed x1, local copies, waits for them, and re-layouts  4.86 us

commit v1 on v0

v1 whole, which is shorter than its diff:
```python
import jax
import jax.numpy as jnp
from jax import lax
from jax.experimental import pallas as pl
from jax.experimental.pallas import tpu as pltpu
from jax.sharding import PartitionSpec as P

SWEEPS = 4
MESH_ID = pl.DeviceIdType.MESH
NB = 48
MG = 4
EX = NB + 2 * MG
LANES = 128
CHUNKS = 3
OFF = 4
KI = 24 * 64
KF = EX * EX - KI
SIDES = ((-1, 0), (1, 0), (0, -1), (0, 1))
OPP_SIDE = (1, 0, 3, 2)
CORNERS = ((-1, -1), (-1, 1), (1, -1), (1, 1))
F32 = jnp.float32
BF16 = jnp.bfloat16


def kernel(f_hbm, u_hbm, c_ref, s_hbm, om_ref, out_hbm,
           SI, SA, SF, Z, R, W, U, C, FX, FY, FE, ces, cer, zes, zer, frs, frr, crs, crr,
           sem_f, sem_u, sem_s, sem_o, sem_cs, sem_cr, sem_zs, sem_zr,
           sem_fs, sem_fr, sem_ks, sem_kr, sem_es, sem_er):
    row = lax.axis_index("row")
    col = lax.axis_index("col")
    has_side = (row > 0, row < 3, col > 0, col < 3)
    has_corner = tuple(
        jnp.logical_and(has_side[0] if dr < 0 else has_side[1], has_side[2] if dc < 0 else has_side[3])
        for dr, dc in CORNERS)

    def dev(delta):
        return {"row": row + delta[0], "col": col + delta[1]}

    def ext_col(j):
        return pl.ds(OFF + EX * MG + j, NB, stride=EX)

    def own_row(i):
        return pl.ds(pl.multiple_of(OFF + EX * (MG + i) + MG, 8), NB)

    def u_copy(s, h):
        return pltpu.make_async_copy(u_hbm.at[s, :, :, pl.ds(h * LANES, LANES)], Z.at[s, h, pl.ds(1, NB), pl.ds(8, NB), :], sem_u.at[s, h])

    def f_copy(s, h):
        return pltpu.make_async_copy(f_hbm.at[s, :, :, pl.ds(h * LANES, LANES)], U.at[s, h], sem_f.at[s, h])

    rows_per = NB * NB // CHUNKS

    mid = pl.ds(2, 24)

    def s_copies(s):
        parts = (
            (s_hbm.at[s, mid, pl.ds(1, 2)], SI.at[s, :, pl.ds(0, 2)]),
            (s_hbm.at[s, mid, pl.ds(4, 2)], SI.at[s, :, pl.ds(2, 2)]),
            (s_hbm.at[s, pl.ds(0, 2)], SA.at[s, pl.ds(0, 2)]),
            (s_hbm.at[s, pl.ds(26, 2)], SA.at[s, pl.ds(2, 2)]),
            (s_hbm.at[s, mid, pl.ds(0, 1)], SF.at[s, :, pl.ds(0, 1)]),
            (s_hbm.at[s, mid, pl.ds(3, 1)], SF.at[s, :, pl.ds(1, 1)]),
            (s_hbm.at[s, mid, pl.ds(6, 1)], SF.at[s, :, pl.ds(2, 1)]))
        return [pltpu.make_async_copy(src, dst, sem_s.at[s, m]) for m, (src, dst) in enumerate(parts)]

    def o_copy(s, h, m):
        g = NB // CHUNKS
        return pltpu.make_async_copy(U.at[s, h, pl.ds(m * g, g)], out_hbm.at[s, pl.ds(m * g, g), :, pl.ds(h * LANES, LANES)], sem_o.at[s, h, m])

    for s in range(2):
        for h in range(2):
            u_copy(s, h).start()
    for s in range(2):
        for h in range(2):
            f_copy(s, h).start()
    for s in range(2):
        for cp in s_copies(s):
            cp.start()

    barrier = pltpu.get_barrier_semaphore()
    n_side = sum(h.astype(jnp.int32) for h in has_side) + sum(h.astype(jnp.int32) for h in has_corner)
    for cond, delta in zip(has_side + has_corner, SIDES + CORNERS):
        @pl.when(cond)
        def _(delta=delta):
            pl.semaphore_signal(barrier, inc=1, device_id=dev(delta), device_id_type=MESH_ID)

    for s in range(2):
        c_t = c_ref[s].T
        for i in range(NB):
            C[s, i, 8:EX, :] = jnp.broadcast_to(c_t[:, i:i + 1], (NB, LANES))

    zero_row = jnp.zeros((64, LANES), F32)

    def zero_z(s, h):
        Z[s, h, 0, :, :] = zero_row
        Z[s, h, 49, :, :] = zero_row

        @pl.loop(1, 49)
        def _(i):
            Z[s, h, i, 0:8, :] = jnp.zeros((8, LANES), F32)
            Z[s, h, i, EX:64, :] = jnp.zeros((8, LANES), F32)

    for s in range(2):
        for h in range(2):
            zero_z(s, h)

    @pl.loop(0, 57)
    def _(i):
        for s in range(2):
            for h in range(2):
                R[s, h, pl.ds(pl.multiple_of(EX * i, 8), EX), :] = jnp.zeros((EX, LANES), F32)

    for s in range(2):
        ces[0, s] = C[s, 0, 8:EX, :]
        ces[1, s] = C[s, NB - 1, 8:EX, :]
        ces[2, s] = C[s, :, 8, :]
        ces[3, s] = C[s, :, EX - 1, :]

    pl.semaphore_wait(barrier, n_side)

    def c_send(d):
        return pltpu.make_async_remote_copy(ces.at[d], cer.at[OPP_SIDE[d]], sem_cs.at[d], sem_cr.at[OPP_SIDE[d]], device_id=dev(SIDES[d]), device_id_type=MESH_ID)

    def c_recv(d):
        return pltpu.make_async_remote_copy(ces.at[OPP_SIDE[d]], cer.at[d], sem_cs.at[OPP_SIDE[d]], sem_cr.at[d], device_id=dev(SIDES[d]), device_id_type=MESH_ID)

    for d in range(4):
        @pl.when(has_side[d])
        def _(d=d):
            c_send(d).start()

    def remote(src, dst, ssem, rsem, delta):
        return pltpu.make_async_remote_copy(src, dst, ssem, rsem, device_id=dev(delta), device_id_type=MESH_ID)

    def z_copy(s, d, slot):
        return remote(zes.at[s, d], zer.at[s, slot], sem_zs.at[s, d], sem_zr.at[s, slot], SIDES[d])

    def z_send(s, d):
        return z_copy(s, d, OPP_SIDE[d])

    def z_recv(s, d):
        return z_copy(s, OPP_SIDE[d], d)

    def early_layers(d):
        return pl.ds(1, 3) if d == 2 else pl.ds(0, 3)

    def late_layers(d):
        return (pl.ds(0, 4), pl.ds(0, 4), pl.ds(0, 1), pl.ds(3, 1))[d]

    def e_copy(s, d, slot, p):
        lay = early_layers(d)
        return remote(frs.at[s, d, lay], frr.at[p, s, slot, lay], sem_es.at[s, d], sem_er.at[p, s, slot], SIDES[d])

    def f_copy_remote(s, d, slot, p):
        lay = late_layers(d)
        return remote(frs.at[s, d, lay], frr.at[p, s, slot, lay], sem_fs.at[s, d], sem_fr.at[p, s, slot], SIDES[d])

    def k_copy(s, q, slot, p):
        return remote(crs.at[s, q], crr.at[p, s, slot], sem_ks.at[s, q], sem_kr.at[p, s, slot], CORNERS[q])

    def when_all(conds, body, order=None):
        for i in (order or range(len(conds))):
            @pl.when(conds[i])
            def _(i=i):
                body(i)

    COLS = (2, 3)
    ROWS = (0, 1)

    def send_z_edges(s, again):
        if again:
            when_all(has_side, lambda d: z_send(s, d).wait_send())
        for h in range(2):
            zes[s, 2, h] = Z[s, h, 1:NB + 1, 8, :]
            zes[s, 3, h] = Z[s, h, 1:NB + 1, EX - 1, :]
        for h in range(2):
            zes[s, 0, h] = Z[s, h, 1, 8:EX, :]
            zes[s, 1, h] = Z[s, h, NB, 8:EX, :]
        when_all(has_side, lambda d: z_send(s, d).start(), COLS + ROWS)

    def stencil(s, om, first):
        @pl.loop(0, NB)
        def _(i):
            ax0 = FX[s, i, :, :]
            ax1 = FX[s, i + 1, :, :]
            ay0 = FY[s, i, 0:NB, :]
            ay1 = FY[s, i, 1:NB + 1, :]
            for h in range(2):
                zc = Z[s, h, i + 1, 8:EX, :]
                zl = Z[s, h, i + 1, 7:EX - 1, :]
                zr = Z[s, h, i + 1, 9:EX + 1, :]
                zu = Z[s, h, i, 8:EX, :]
                zd = Z[s, h, i + 2, 8:EX, :]
                av = ax0 * (zc - zu) - ax1 * (zd - zc) + ay0 * (zc - zl) - ay1 * (zr - zc)
                if first:
                    R[s, h, own_row(i), :] = U[s, h, i] - av
                    U[s, h, i] = zc
                else:
                    R[s, h, own_row(i), :] = R[s, h, own_row(i), :] - om * av
                    U[s, h, i] = U[s, h, i] + om * zc

    def edge_fix(s, om, sides):
        def fix(d):
            z_recv(s, d).wait_recv()
            for h in range(2):
                cells = (own_row(0), own_row(NB - 1), ext_col(MG), ext_col(MG + NB - 1))[d]
                R[s, h, cells, :] = R[s, h, cells, :] + om * (FE[s, d] * zer[s, d, h])
        when_all(has_side, fix, sides)

    def pack_col(s, h, d, a):
        first = MG if d == 2 else NB
        frs[s, d, a, :, pl.ds(h * LANES, LANES)] = R[s, h, ext_col(first + a), :].astype(BF16)

    def send_early(s, p, again):
        if again:
            when_all(has_side, lambda d: e_copy(s, d, OPP_SIDE[d], p).wait_send(), COLS)
        for d in COLS:
            for h in range(2):
                for a in ((1, 2, 3) if d == 2 else (0, 1, 2)):
                    pack_col(s, h, d, a)
        when_all(has_side, lambda d: e_copy(s, d, OPP_SIDE[d], p).start(), COLS)

    def send_late(s, p, again):
        if again:
            when_all(has_side, lambda d: f_copy_remote(s, d, OPP_SIDE[d], p).wait_send())
            when_all(has_corner, lambda q: k_copy(s, q, 3 - q, p).wait_send())
        for h in range(2):
            lanes = pl.ds(h * LANES, LANES)
            pack_col(s, h, 2, 0)
            pack_col(s, h, 3, 3)
            for a in range(MG):
                frs[s, 0, a, :, lanes] = R[s, h, own_row(a), :].astype(BF16)
                frs[s, 1, a, :, lanes] = R[s, h, own_row(NB - MG + a), :].astype(BF16)
            for q, (dr, dc) in enumerate(CORNERS):
                r0 = MG if dr < 0 else NB
                c0 = 0 if dc < 0 else NB
                tile = [R[s, h, pl.ds(OFF + EX * (r0 + a) + c0, 8), :] for a in range(MG)]
                crs[s, q, :, lanes] = jnp.concatenate(tile, axis=0).astype(BF16)
        when_all(has_side, lambda d: f_copy_remote(s, d, OPP_SIDE[d], p).start(), COLS + ROWS)
        when_all(has_corner, lambda q: k_copy(s, q, 3 - q, p).start())

    def recv_frames(s, p):
        def side(d):
            if d in COLS:
                e_copy(s, OPP_SIDE[d], d, p).wait_recv()
            f_copy_remote(s, OPP_SIDE[d], d, p).wait_recv()
            for h in range(2):
                lanes = pl.ds(h * LANES, LANES)
                for a in range(MG):
                    v = frr[p, s, d, a, :, lanes].astype(F32)
                    cells = (own_row(a - MG), own_row(NB + a), ext_col(a), ext_col(MG + NB + a))[d]
                    R[s, h, cells, :] = v

        def corner(q):
            k_copy(s, 3 - q, q, p).wait_recv()
            dr, dc = CORNERS[q]
            r0 = 0 if dr < 0 else MG + NB
            for h in range(2):
                v = crr[p, s, q, :, pl.ds(h * LANES, LANES)].astype(F32)
                for a in range(MG):
                    if dc < 0:
                        R[s, h, pl.ds(OFF + EX * (r0 + a), 4), :] = v[8 * a:8 * a + 4]
                    else:
                        R[s, h, pl.ds(OFF + EX * (r0 + a) + MG + NB, 4), :] = v[8 * a + 4:8 * a + 8]
        when_all(has_side, side)
        when_all(has_corner, corner)

    def pair_rows(s, h, t):
        return R[s, h, pl.ds(2 * EX * t + OFF, 2 * EX), :].astype(BF16)

    def fill_inner(s):
        @pl.loop(2, 26)
        def _(t):
            for h in range(2):
                v = pair_rows(s, h, t)
                for n, u in enumerate((1, 2, 4, 5)):
                    W[s, pl.ds(pl.multiple_of(64 * (t - 2) + 16 * n, 16), 16), pl.ds(h * LANES, LANES)] = v[16 * u:16 * u + 16]

    def fill_frame(s):
        @pl.loop(2, 26)
        def _(t):
            for h in range(2):
                v = pair_rows(s, h, t)
                for n, u in enumerate((0, 3, 6)):
                    W[s, pl.ds(pl.multiple_of(KI + 448 + 48 * (t - 2) + 16 * n, 16), 16), pl.ds(h * LANES, LANES)] = v[16 * u:16 * u + 16]
        for h in range(2):
            for n, t in enumerate((0, 1, 26, 27)):
                W[s, pl.ds(KI + 112 * n, 112), pl.ds(h * LANES, LANES)] = pair_rows(s, h, t)

    g = NB // CHUNKS

    def matmul(s, m, parts, k0):
        cells = pl.ds(m * rows_per, rows_per)
        lhs = [p[s, :, :, :, cells].reshape(-1, rows_per) for p in parts]
        lhs = jnp.concatenate(lhs, axis=0) if len(lhs) > 1 else lhs[0]
        z = lax.dot_general(lhs, W[s, pl.ds(k0, lhs.shape[0]), :], (((0,), (0,)), ((), ())), preferred_element_type=F32)
        return z.reshape(g, NB, 2 * LANES)

    def inner_product(s):
        fill_inner(s)
        for m in range(CHUNKS):
            z = matmul(s, m, (SI,), 0)
            for h in range(2):
                Z[s, h, pl.ds(1 + m * g, g), 8:EX, :] = z[:, :, h * LANES:(h + 1) * LANES]

    def frame_product(s, m):
        z = matmul(s, m, (SA, SF), KI)
        return [Z[s, h, pl.ds(1 + m * g, g), 8:EX, :] + z[:, :, h * LANES:(h + 1) * LANES] for h in range(2)]

    for s in range(2):
        for h in range(2):
            u_copy(s, h).wait()
        send_z_edges(s, False)
    for s in range(2):
        @pl.loop(1, NB)
        def _(i):
            FX[s, i, :, :] = 0.5 * (C[s, i - 1, 8:EX, :] + C[s, i, 8:EX, :])
        C[s, :, 0:8, :] = jnp.zeros((NB, 8, LANES), F32)

        @pl.loop(0, NB)
        def _(i):
            FY[s, i, 0:NB, :] = 0.5 * (C[s, i, 7:EX - 1, :] + C[s, i, 8:EX, :])
    when_all(has_side, lambda d: c_recv(d).wait_recv())
    for s in range(2):
        for d in range(4):
            own = ces[d, s]
            face = jnp.where(has_side[d], 0.5 * (own + cer[d, s]), own)
            if d == 0:
                FX[s, 0, :, :] = face
            elif d == 1:
                FX[s, NB, :, :] = face
            elif d == 2:
                FY[s, :, 0, :] = face
            else:
                FY[s, :, NB, :] = face
            FE[s, d] = face
    for s in range(2):
        for h in range(2):
            f_copy(s, h).wait()
        stencil(s, None, True)
    for s in range(2):
        edge_fix(s, 1.0, ROWS)
        send_early(s, 0, False)
    for s in range(2):
        edge_fix(s, 1.0, COLS)
        send_late(s, 0, False)

    for s in range(2):
        for cp in s_copies(s):
            cp.wait()
        inner_product(s)

    def half_sweep(s, k, p_in, other, p_other, fix_other):
        recv_frames(s, p_in)
        fill_frame(s)
        for m in range(CHUNKS):
            z = frame_product(s, m)
            for h in range(2):
                Z[s, h, pl.ds(1 + m * g, g), 8:EX, :] = z[h]
            if m == 1:
                late(other, p_other, fix_other)
        send_z_edges(s, True)
        stencil(s, om_ref[s], False)

    def late(s, p, wanted):
        @pl.when(wanted)
        def _():
            edge_fix(s, om_ref[s], COLS)
            send_late(s, p, True)

    @pl.loop(0, SWEEPS - 1)
    def _(k):
        p = lax.rem(k, 2)
        half_sweep(0, k, p, 1, p, k > 0)

        @pl.when(k > 0)
        def _():
            inner_product(1)
        edge_fix(0, om_ref[0], ROWS)
        send_early(0, 1 - p, True)
        half_sweep(1, k, p, 0, 1 - p, k >= 0)
        inner_product(0)
        edge_fix(1, om_ref[1], ROWS)
        send_early(1, 1 - p, True)

    last = (SWEEPS - 1) % 2

    def finish(s, m):
        z = frame_product(s, m)
        for h in range(2):
            U[s, h, pl.ds(m * g, g)] = U[s, h, pl.ds(m * g, g)] + om_ref[s] * z[h]
            o_copy(s, h, m).start()

    recv_frames(0, last)
    fill_frame(0)
    for m in range(CHUNKS):
        finish(0, m)
        if m == 1:
            late(1, last, row >= 0)
    inner_product(1)
    recv_frames(1, last)
    fill_frame(1)
    for m in range(CHUNKS):
        finish(1, m)
    when_all(has_side, lambda d: c_send(d).wait_send())
    for s in range(2):
        when_all(has_side, lambda d: z_send(s, d).wait_send())
        when_all(has_side, lambda d: e_copy(s, d, OPP_SIDE[d], last).wait_send(), COLS)
        when_all(has_side, lambda d: f_copy_remote(s, d, OPP_SIDE[d], last).wait_send())
        when_all(has_corner, lambda q: k_copy(s, q, 3 - q, last).wait_send())
        for h in range(2):
            for m in range(CHUNKS):
                o_copy(s, h, m).wait()


def solution(mesh):
    grid_spec = P(None, "row", "col", None)

    def local(forcing, init_guess, cell_coef, solve_rows, relax_factor):
        num_sys, nb, _, rhs = forcing.shape
        s_mat = jnp.swapaxes(solve_rows, 3, 4).reshape(num_sys, EX // 2, 7, 16, nb * nb)
        any_spec = pl.BlockSpec(memory_space=pl.ANY)
        dma = pltpu.SemaphoreType.DMA
        return pl.pallas_call(
            kernel,
            name="schwarz",
            out_shape=jax.ShapeDtypeStruct(forcing.shape, F32),
            in_specs=[any_spec, any_spec, pl.BlockSpec(memory_space=pltpu.VMEM), any_spec, pl.BlockSpec(memory_space=pltpu.SMEM)],
            out_specs=any_spec,
            scratch_shapes=[
                pltpu.VMEM((2, 24, 4, 16, NB * NB), BF16),
                pltpu.VMEM((2, 4, 7, 16, NB * NB), BF16),
                pltpu.VMEM((2, 24, 3, 16, NB * NB), BF16),
                pltpu.VMEM((2, 2, 50, 64, LANES), F32),
                pltpu.VMEM((2, 2, 57 * EX, LANES), F32),
                pltpu.VMEM((2, EX * EX, 2 * LANES), BF16),
                pltpu.VMEM((2, 2, NB, NB, LANES), F32),
                pltpu.VMEM((2, NB, EX, LANES), F32),
                pltpu.VMEM((2, NB + 1, NB, LANES), F32),
                pltpu.VMEM((2, NB, EX, LANES), F32),
                pltpu.VMEM((2, 4, NB, LANES), F32),
                pltpu.VMEM((4, 2, NB, LANES), F32),
                pltpu.VMEM((4, 2, NB, LANES), F32),
                pltpu.VMEM((2, 4, 2, NB, LANES), F32),
                pltpu.VMEM((2, 4, 2, NB, LANES), F32),
                pltpu.VMEM((2, 4, MG, NB, 2 * LANES), BF16),
                pltpu.VMEM((2, 2, 4, MG, NB, 2 * LANES), BF16),
                pltpu.VMEM((2, 4, 32, 2 * LANES), BF16),
                pltpu.VMEM((2, 2, 4, 32, 2 * LANES), BF16),
                dma((2, 2)), dma((2, 2)), dma((2, 7)), dma((2, 2, CHUNKS)),
                dma((4,)), dma((4,)), dma((2, 4)), dma((2, 4)),
                dma((2, 4)), dma((2, 2, 4)), dma((2, 4)), dma((2, 2, 4)), dma((2, 4)), dma((2, 2, 4)),
            ],
            compiler_params=pltpu.CompilerParams(collective_id=0, has_side_effects=True, vmem_limit_bytes=66_000_000),
            cost_estimate=pl.CostEstimate(flops=30_000_000_000, bytes_accessed=43_000_000, transcendentals=0),
        )(forcing, init_guess, cell_coef, s_mat, relax_factor)

    return jax.shard_map(local, mesh=mesh, in_specs=(grid_spec, grid_spec, P(None, "row", "col"), P(None, "row", "col", None, None), P(None)), out_specs=grid_spec, check_vma=False)
```

time: 104 us -> 94.4 us (0.908)
  Pallas kernels: 98.7 us -> 89.4 us
    pallas_call x1, Pallas kernels: 98.7 us -> 89.4 us  [local(): pl.pallas_call(kernel, name='schwarz', out_shape=jax.ShapeDtypeStruct(for...]
where the time goes in v1:
time: 94.4 us; the launch traced here: 94.3 us
  Pallas kernels  89.4 us (95%)
  local copies, waits for them, and re-layouts  4.86 us (5%)
    pallas_call x1, Pallas kernels, local(): pl.pallas_call(kernel, name='schwarz', out_shape=jax.ShapeDtypeStruct(for...  89.4 us
    unnamed x1, local copies, waits for them, and re-layouts  4.86 us

profile of v1, /device:TPU:0, one launch (start us, length us, event | category | flops | bytes accessed | tf_op | source)
XLA Modules:
  0.0 94.3 jit_solution(16631393708579683819)
XLA Ops:
  0.0 89.4 %schwarz.1 = f32[2,48,48,256]{3,2,1,0:T(8,128)} custom-call(f32[2,48,48,256]{3,2,1,0:T(8,128)} %f_hbm.1, f32[2,48,48,256]{3,2,1,0:T(8,128)} %u_hbm.1, f32[2,48,48]{2,1,0:T(8,128)} %c_ref.1, bf16[2,28,7,16,2304]{4,3,2,1,0:T(8,128)(2,1)} %bitcast.3, f32[2]{0:T(128)} %om_ref.1), custom_call_target="tpu_custom_call" | custom-call | flops 30000001024 | bytes 43000000 | tf_op jit(solution)/shard_map/schwarz/pallas_call | solution.py:424
  89.4 4.9 %copy.7 = f32[2,48,48,256]{3,2,1,0:T(8,128)} copy(f32[2,48,48,256]{3,2,1,0:T(8,128)} %schwarz.1) | data formatting | bytes 9437184

commit v2 on v1

--- a/solution.py
+++ b/solution.py
@@ -12,6 +12,7 @@
 EX = NB + 2 * MG
 LANES = 128
 CHUNKS = 3
+LATE_AT = 1
 OFF = 4
 KI = 24 * 64
 KF = EX * EX - KI
@@ -23,7 +24,7 @@
 
 
 def kernel(f_hbm, u_hbm, c_ref, s_hbm, om_ref, out_hbm,
-           SI, SA, SF, Z, R, W, U, C, FX, FY, FE, ces, cer, zes, zer, frs, frr, crs, crr,
+           SI, SA, SF, Z, R, W, U, FX, FY, FE, ces, cer, zes, zer, frs, frr, crs, crr,
            sem_f, sem_u, sem_s, sem_o, sem_cs, sem_cr, sem_zs, sem_zr,
            sem_fs, sem_fr, sem_ks, sem_kr, sem_es, sem_er):
     row = lax.axis_index("row")
@@ -40,7 +41,8 @@
         return pl.ds(OFF + EX * MG + j, NB, stride=EX)
 
     def own_row(i):
-        return pl.ds(pl.multiple_of(OFF + EX * (MG + i) + MG, 8), NB)
+        start = OFF + EX * (MG + i) + MG
+        return pl.ds(start if isinstance(i, int) else pl.multiple_of(start, 8), NB)
 
     def u_copy(s, h):
         return pltpu.make_async_copy(u_hbm.at[s, :, :, pl.ds(h * LANES, LANES)], Z.at[s, h, pl.ds(1, NB), pl.ds(8, NB), :], sem_u.at[s, h])
@@ -52,7 +54,7 @@
 
     mid = pl.ds(2, 24)
 
-    def s_copies(s):
+    def s_copies(s, inner):
         parts = (
             (s_hbm.at[s, mid, pl.ds(1, 2)], SI.at[s, :, pl.ds(0, 2)]),
             (s_hbm.at[s, mid, pl.ds(4, 2)], SI.at[s, :, pl.ds(2, 2)]),
@@ -61,7 +63,7 @@
             (s_hbm.at[s, mid, pl.ds(0, 1)], SF.at[s, :, pl.ds(0, 1)]),
             (s_hbm.at[s, mid, pl.ds(3, 1)], SF.at[s, :, pl.ds(1, 1)]),
             (s_hbm.at[s, mid, pl.ds(6, 1)], SF.at[s, :, pl.ds(2, 1)]))
-        return [pltpu.make_async_copy(src, dst, sem_s.at[s, m]) for m, (src, dst) in enumerate(parts)]
+        return [pltpu.make_async_copy(src, dst, sem_s.at[s, m]) for m, (src, dst) in enumerate(parts) if (m < 2) == inner]
 
     def o_copy(s, h, m):
         g = NB // CHUNKS
@@ -73,9 +75,10 @@
     for s in range(2):
         for h in range(2):
             f_copy(s, h).start()
-    for s in range(2):
-        for cp in s_copies(s):
-            cp.start()
+    for first in (True, False):
+        for s in range(2):
+            for cp in s_copies(s, first):
+                cp.start()
 
     barrier = pltpu.get_barrier_semaphore()
     n_side = sum(h.astype(jnp.int32) for h in has_side) + sum(h.astype(jnp.int32) for h in has_corner)
@@ -87,7 +90,7 @@
     for s in range(2):
         c_t = c_ref[s].T
         for i in range(NB):
-            C[s, i, 8:EX, :] = jnp.broadcast_to(c_t[:, i:i + 1], (NB, LANES))
+            R[s, 0, pl.ds(EX * i + 8, NB), :] = jnp.broadcast_to(c_t[:, i:i + 1], (NB, LANES))
 
     zero_row = jnp.zeros((64, LANES), F32)
 
@@ -104,17 +107,25 @@
         for h in range(2):
             zero_z(s, h)
 
-    @pl.loop(0, 57)
-    def _(i):
-        for s in range(2):
-            for h in range(2):
-                R[s, h, pl.ds(pl.multiple_of(EX * i, 8), EX), :] = jnp.zeros((EX, LANES), F32)
-
-    for s in range(2):
-        ces[0, s] = C[s, 0, 8:EX, :]
-        ces[1, s] = C[s, NB - 1, 8:EX, :]
-        ces[2, s] = C[s, :, 8, :]
-        ces[3, s] = C[s, :, EX - 1, :]
+    for d in range(4):
+        @pl.when(jnp.logical_not(has_side[d]))
+        def _(d=d):
+            for s in range(2):
+                zer[s, d] = jnp.zeros((2, NB, LANES), F32)
+                for p in range(2):
+                    frr[p, s, d] = jnp.zeros((MG, NB, 2 * LANES), BF16)
+    for q in range(4):
+        @pl.when(jnp.logical_not(has_corner[q]))
+        def _(q=q):
+            for s in range(2):
+                for p in range(2):
+                    crr[p, s, q] = jnp.zeros((32, 2 * LANES), BF16)
+
+    for s in range(2):
+        ces[0, s] = R[s, 0, pl.ds(8, NB), :]
+        ces[1, s] = R[s, 0, pl.ds(EX * (NB - 1) + 8, NB), :]
+        ces[2, s] = R[s, 0, pl.ds(8, NB, stride=EX), :]
+        ces[3, s] = R[s, 0, pl.ds(EX - 1, NB, stride=EX), :]
 
     pl.semaphore_wait(barrier, n_side)
 
@@ -199,13 +210,26 @@
                     R[s, h, own_row(i), :] = R[s, h, own_row(i), :] - om * av
                     U[s, h, i] = U[s, h, i] + om * zc
 
+    def stencil_rows(s, om, rows):
+        for h in range(2):
+            zc = Z[s, h, rows[0] + 1, 8:EX, :]
+            flux = FX[s, rows[0], :, :] * (zc - Z[s, h, rows[0], 8:EX, :])
+            for i in rows:
+                zd = Z[s, h, i + 2, 8:EX, :]
+                down = FX[s, i + 1, :, :] * (zd - zc)
+                side = FY[s, i, 0:NB, :] * (zc - Z[s, h, i + 1, 7:EX - 1, :]) - FY[s, i, 1:NB + 1, :] * (Z[s, h, i + 1, 9:EX + 1, :] - zc)
+                R[s, h, own_row(i), :] = R[s, h, own_row(i), :] - om * ((flux - down) + side)
+                U[s, h, i] = U[s, h, i] + om * zc
+                flux, zc = down, zd
+
+    def wait_z(s, sides):
+        when_all(has_side, lambda d: z_recv(s, d).wait_recv(), sides)
+
     def edge_fix(s, om, sides):
-        def fix(d):
-            z_recv(s, d).wait_recv()
+        for d in sides:
             for h in range(2):
                 cells = (own_row(0), own_row(NB - 1), ext_col(MG), ext_col(MG + NB - 1))[d]
                 R[s, h, cells, :] = R[s, h, cells, :] + om * (FE[s, d] * zer[s, d, h])
-        when_all(has_side, fix, sides)
 
     def pack_col(s, h, d, a):
         first = MG if d == 2 else NB
@@ -239,21 +263,18 @@
         when_all(has_side, lambda d: f_copy_remote(s, d, OPP_SIDE[d], p).start(), COLS + ROWS)
         when_all(has_corner, lambda q: k_copy(s, q, 3 - q, p).start())
 
-    def recv_frames(s, p):
-        def side(d):
-            if d in COLS:
-                e_copy(s, OPP_SIDE[d], d, p).wait_recv()
-            f_copy_remote(s, OPP_SIDE[d], d, p).wait_recv()
-            for h in range(2):
-                lanes = pl.ds(h * LANES, LANES)
+    def wait_frames(s, p):
+        when_all(has_side, lambda d: e_copy(s, OPP_SIDE[d], d, p).wait_recv(), COLS)
+        when_all(has_side, lambda d: f_copy_remote(s, OPP_SIDE[d], d, p).wait_recv())
+        when_all(has_corner, lambda q: k_copy(s, 3 - q, q, p).wait_recv())
+
+    def scatter_frames(s, p):
+        for d in range(4):
+            for h in range(2):
                 for a in range(MG):
-                    v = frr[p, s, d, a, :, lanes].astype(F32)
                     cells = (own_row(a - MG), own_row(NB + a), ext_col(a), ext_col(MG + NB + a))[d]
-                    R[s, h, cells, :] = v
-
-        def corner(q):
-            k_copy(s, 3 - q, q, p).wait_recv()
-            dr, dc = CORNERS[q]
+                    R[s, h, cells, :] = frr[p, s, d, a, :, pl.ds(h * LANES, LANES)].astype(F32)
+        for q, (dr, dc) in enumerate(CORNERS):
             r0 = 0 if dr < 0 else MG + NB
             for h in range(2):
                 v = crr[p, s, q, :, pl.ds(h * LANES, LANES)].astype(F32)
@@ -262,30 +283,26 @@
                         R[s, h, pl.ds(OFF + EX * (r0 + a), 4), :] = v[8 * a:8 * a + 4]
                     else:
                         R[s, h, pl.ds(OFF + EX * (r0 + a) + MG + NB, 4), :] = v[8 * a + 4:8 * a + 8]
-        when_all(has_side, side)
-        when_all(has_corner, corner)
 
     def pair_rows(s, h, t):
         return R[s, h, pl.ds(2 * EX * t + OFF, 2 * EX), :].astype(BF16)
 
+    def fill(s, t, tile, n, base):
+        for h in range(2):
+            v = R[s, h, pl.ds(2 * EX * t + 16 * tile + OFF, 16 * n), :].astype(BF16)
+            W[s, pl.ds(base, 16 * n), pl.ds(h * LANES, LANES)] = v
+
     def fill_inner(s):
-        @pl.loop(2, 26)
-        def _(t):
-            for h in range(2):
-                v = pair_rows(s, h, t)
-                for n, u in enumerate((1, 2, 4, 5)):
-                    W[s, pl.ds(pl.multiple_of(64 * (t - 2) + 16 * n, 16), 16), pl.ds(h * LANES, LANES)] = v[16 * u:16 * u + 16]
+        for t in range(2, 26):
+            fill(s, t, 1, 2, 64 * (t - 2))
+            fill(s, t, 4, 2, 64 * (t - 2) + 32)
 
     def fill_frame(s):
-        @pl.loop(2, 26)
-        def _(t):
-            for h in range(2):
-                v = pair_rows(s, h, t)
-                for n, u in enumerate((0, 3, 6)):
-                    W[s, pl.ds(pl.multiple_of(KI + 448 + 48 * (t - 2) + 16 * n, 16), 16), pl.ds(h * LANES, LANES)] = v[16 * u:16 * u + 16]
-        for h in range(2):
-            for n, t in enumerate((0, 1, 26, 27)):
-                W[s, pl.ds(KI + 112 * n, 112), pl.ds(h * LANES, LANES)] = pair_rows(s, h, t)
+        fill(s, 0, 0, 14, KI)
+        fill(s, 26, 0, 14, KI + 224)
+        for t in range(2, 26):
+            for n, u in enumerate((0, 3, 6)):
+                fill(s, t, u, 1, KI + 448 + 48 * (t - 2) + 16 * n)
 
     g = NB // CHUNKS
 
@@ -296,9 +313,11 @@
         z = lax.dot_general(lhs, W[s, pl.ds(k0, lhs.shape[0]), :], (((0,), (0,)), ((), ())), preferred_element_type=F32)
         return z.reshape(g, NB, 2 * LANES)
 
-    def inner_product(s):
+    def inner_product(s, other=None):
         fill_inner(s)
         for m in range(CHUNKS):
+            if other is not None:
+                stencil_rows(other, om_ref[other], range(m * g, (m + 1) * g))
             z = matmul(s, m, (SI,), 0)
             for h in range(2):
                 Z[s, h, pl.ds(1 + m * g, g), 8:EX, :] = z[:, :, h * LANES:(h + 1) * LANES]
@@ -312,14 +331,22 @@
             u_copy(s, h).wait()
         send_z_edges(s, False)
     for s in range(2):
-        @pl.loop(1, NB)
-        def _(i):
-            FX[s, i, :, :] = 0.5 * (C[s, i - 1, 8:EX, :] + C[s, i, 8:EX, :])
-        C[s, :, 0:8, :] = jnp.zeros((NB, 8, LANES), F32)
+        for i in range(NB):
+            R[s, 0, pl.ds(EX * i, 8), :] = jnp.zeros((8, LANES), F32)
 
         @pl.loop(0, NB)
         def _(i):
-            FY[s, i, 0:NB, :] = 0.5 * (C[s, i, 7:EX - 1, :] + C[s, i, 8:EX, :])
+            at = pl.multiple_of(EX * i, 8)
+            c_own = R[s, 0, pl.ds(at + 8, NB), :]
+            FX[s, i + 1, :, :] = 0.5 * (c_own + R[s, 0, pl.ds(at + EX + 8, NB), :])
+            FY[s, i, 0:NB, :] = 0.5 * (c_own + R[s, 0, pl.ds(at + 7, NB), :])
+
+    @pl.loop(0, 57)
+    def _(i):
+        for s in range(2):
+            for h in range(2):
+                R[s, h, pl.ds(pl.multiple_of(EX * i, 8), EX), :] = jnp.zeros((EX, LANES), F32)
+
     when_all(has_side, lambda d: c_recv(d).wait_recv())
     for s in range(2):
         for d in range(4):
@@ -338,50 +365,60 @@
         for h in range(2):
             f_copy(s, h).wait()
         stencil(s, None, True)
-    for s in range(2):
-        edge_fix(s, 1.0, ROWS)
+        wait_z(s, ROWS + COLS)
+        edge_fix(s, 1.0, ROWS + COLS)
         send_early(s, 0, False)
-    for s in range(2):
-        edge_fix(s, 1.0, COLS)
         send_late(s, 0, False)
 
     for s in range(2):
-        for cp in s_copies(s):
+        for cp in s_copies(s, True):
             cp.wait()
         inner_product(s)
-
-    def half_sweep(s, k, p_in, other, p_other, fix_other):
-        recv_frames(s, p_in)
+    for s in range(2):
+        for cp in s_copies(s, False):
+            cp.wait()
+
+    def early(s, p):
+        wait_z(s, ROWS)
+        edge_fix(s, om_ref[s], ROWS)
+        send_early(s, p, True)
+
+    def late(s, p):
+        wait_z(s, COLS)
+        edge_fix(s, om_ref[s], COLS)
+        send_late(s, p, True)
+
+    def half_sweep(s, p, other, p_other, started):
+        @pl.when(started)
+        def _():
+            early(other, p_other)
+        wait_frames(s, p)
+        scatter_frames(s, p)
         fill_frame(s)
         for m in range(CHUNKS):
             z = frame_product(s, m)
             for h in range(2):
                 Z[s, h, pl.ds(1 + m * g, g), 8:EX, :] = z[h]
-            if m == 1:
-                late(other, p_other, fix_other)
+            if m == LATE_AT:
+                @pl.when(started)
+                def _():
+                    late(other, p_other)
         send_z_edges(s, True)
-        stencil(s, om_ref[s], False)
-
-    def late(s, p, wanted):
-        @pl.when(wanted)
-        def _():
-            edge_fix(s, om_ref[s], COLS)
-            send_late(s, p, True)
 
     @pl.loop(0, SWEEPS - 1)
     def _(k):
         p = lax.rem(k, 2)
-        half_sweep(0, k, p, 1, p, k > 0)
+        half_sweep(0, p, 1, p, k > 0)
 
         @pl.when(k > 0)
         def _():
-            inner_product(1)
-        edge_fix(0, om_ref[0], ROWS)
-        send_early(0, 1 - p, True)
-        half_sweep(1, k, p, 0, 1 - p, k >= 0)
-        inner_product(0)
-        edge_fix(1, om_ref[1], ROWS)
-        send_early(1, 1 - p, True)
+            inner_product(1, 0)
+
+        @pl.when(k == 0)
+        def _():
+            stencil(0, om_ref[0], False)
+        half_sweep(1, p, 0, 1 - p, k >= 0)
+        inner_product(0, 1)
 
     last = (SWEEPS - 1) % 2
 
@@ -389,19 +426,28 @@
         z = frame_product(s, m)
         for h in range(2):
             U[s, h, pl.ds(m * g, g)] = U[s, h, pl.ds(m * g, g)] + om_ref[s] * z[h]
-            o_copy(s, h, m).start()
-
-    recv_frames(0, last)
+
+    def write_out(s):
+        for h in range(2):
+            for m in range(CHUNKS):
+                o_copy(s, h, m).start()
+
+    early(1, last)
+    wait_frames(0, last)
+    scatter_frames(0, last)
     fill_frame(0)
     for m in range(CHUNKS):
         finish(0, m)
-        if m == 1:
-            late(1, last, row >= 0)
+        if m == LATE_AT:
+            late(1, last)
+    write_out(0)
     inner_product(1)
-    recv_frames(1, last)
+    wait_frames(1, last)
+    scatter_frames(1, last)
     fill_frame(1)
     for m in range(CHUNKS):
         finish(1, m)
+    write_out(1)
     when_all(has_side, lambda d: c_send(d).wait_send())
     for s in range(2):
         when_all(has_side, lambda d: z_send(s, d).wait_send())
@@ -435,7 +481,6 @@
                 pltpu.VMEM((2, 2, 57 * EX, LANES), F32),
                 pltpu.VMEM((2, EX * EX, 2 * LANES), BF16),
                 pltpu.VMEM((2, 2, NB, NB, LANES), F32),
-                pltpu.VMEM((2, NB, EX, LANES), F32),
                 pltpu.VMEM((2, NB + 1, NB, LANES), F32),
                 pltpu.VMEM((2, NB, EX, LANES), F32),
                 pltpu.VMEM((2, 4, NB, LANES), F32),

time: 94.4 us -> 84.8 us (0.90)
  Pallas kernels: 89.4 us -> 79.7 us
    pallas_call x1, Pallas kernels: 89.4 us -> 79.7 us  [local(): pl.pallas_call(kernel, name='schwarz', out_shape=jax.ShapeDtypeStruct(for...]
where the time goes in v2:
time: 84.8 us; the launch traced here: 84.6 us
  Pallas kernels  79.7 us (94%)
  local copies, waits for them, and re-layouts  4.86 us (6%)
    pallas_call x1, Pallas kernels, local(): pl.pallas_call(kernel, name='schwarz', out_shape=jax.ShapeDtypeStruct(for...  79.7 us
    unnamed x1, local copies, waits for them, and re-layouts  4.86 us

profile of v2, /device:TPU:0, one launch (start us, length us, event | category | flops | bytes accessed | tf_op | source)
XLA Modules:
  0.0 84.6 jit_solution(2602725021340473055)
XLA Ops:
  0.0 79.7 %schwarz.1 = f32[2,48,48,256]{3,2,1,0:T(8,128)} custom-call(f32[2,48,48,256]{3,2,1,0:T(8,128)} %f_hbm.1, f32[2,48,48,256]{3,2,1,0:T(8,128)} %u_hbm.1, f32[2,48,48]{2,1,0:T(8,128)} %c_ref.1, bf16[2,28,7,16,2304]{4,3,2,1,0:T(8,128)(2,1)} %bitcast.3, f32[2]{0:T(128)} %om_ref.1), custom_call_target="tpu_custom_call" | custom-call | flops 30000001024 | bytes 43000000 | tf_op jit(solution)/shard_map/schwarz/pallas_call | solution.py:470
  79.7 4.9 %copy.7 = f32[2,48,48,256]{3,2,1,0:T(8,128)} copy(f32[2,48,48,256]{3,2,1,0:T(8,128)} %schwarz.1) | data formatting | bytes 9437184

commit v3 on v2

--- a/solution.py
+++ b/solution.py
@@ -12,7 +12,7 @@
 EX = NB + 2 * MG
 LANES = 128
 CHUNKS = 3
-LATE_AT = 1
+LATE_AT = 2
 OFF = 4
 KI = 24 * 64
 KF = EX * EX - KI
@@ -23,9 +23,9 @@
 BF16 = jnp.bfloat16
 
 
-def kernel(f_hbm, u_hbm, c_ref, s_hbm, om_ref, out_hbm,
-           SI, SA, SF, Z, R, W, U, FX, FY, FE, ces, cer, zes, zer, frs, frr, crs, crr,
-           sem_f, sem_u, sem_s, sem_o, sem_cs, sem_cr, sem_zs, sem_zr,
+def kernel(f_hbm, u_hbm, c_hbm, s_hbm, om_ref, U,
+           c_ref, SI, SA, SF, Z, R, W, FX, FY, FE, ces, cer, zes, zer, frs, frr, crs, crr,
+           sem_c, sem_f, sem_u, sem_s, sem_cs, sem_cr, sem_zs, sem_zr,
            sem_fs, sem_fr, sem_ks, sem_kr, sem_es, sem_er):
     row = lax.axis_index("row")
     col = lax.axis_index("col")
@@ -65,20 +65,14 @@
             (s_hbm.at[s, mid, pl.ds(6, 1)], SF.at[s, :, pl.ds(2, 1)]))
         return [pltpu.make_async_copy(src, dst, sem_s.at[s, m]) for m, (src, dst) in enumerate(parts) if (m < 2) == inner]
 
-    def o_copy(s, h, m):
-        g = NB // CHUNKS
-        return pltpu.make_async_copy(U.at[s, h, pl.ds(m * g, g)], out_hbm.at[s, pl.ds(m * g, g), :, pl.ds(h * LANES, LANES)], sem_o.at[s, h, m])
-
+    c_copy = pltpu.make_async_copy(c_hbm, c_ref, sem_c)
+    c_copy.start()
     for s in range(2):
         for h in range(2):
             u_copy(s, h).start()
     for s in range(2):
         for h in range(2):
             f_copy(s, h).start()
-    for first in (True, False):
-        for s in range(2):
-            for cp in s_copies(s, first):
-                cp.start()
 
     barrier = pltpu.get_barrier_semaphore()
     n_side = sum(h.astype(jnp.int32) for h in has_side) + sum(h.astype(jnp.int32) for h in has_corner)
@@ -87,6 +81,7 @@
         def _(delta=delta):
             pl.semaphore_signal(barrier, inc=1, device_id=dev(delta), device_id_type=MESH_ID)
 
+    c_copy.wait()
     for s in range(2):
         c_t = c_ref[s].T
         for i in range(NB):
@@ -112,6 +107,7 @@
         def _(d=d):
             for s in range(2):
                 zer[s, d] = jnp.zeros((2, NB, LANES), F32)
+                cer[d, s] = jnp.zeros((NB, LANES), F32)
                 for p in range(2):
                     frr[p, s, d] = jnp.zeros((MG, NB, 2 * LANES), BF16)
     for q in range(4):
@@ -229,7 +225,7 @@
         for d in sides:
             for h in range(2):
                 cells = (own_row(0), own_row(NB - 1), ext_col(MG), ext_col(MG + NB - 1))[d]
-                R[s, h, cells, :] = R[s, h, cells, :] + om * (FE[s, d] * zer[s, d, h])
+                R[s, h, cells, :] = R[s, h, cells, :] + om * (FE[s, d] * (zer[s, d, h] - zes[s, d, h]))
 
     def pack_col(s, h, d, a):
         first = MG if d == 2 else NB
@@ -330,6 +326,10 @@
         for h in range(2):
             u_copy(s, h).wait()
         send_z_edges(s, False)
+    for first in (True, False):
+        for s in range(2):
+            for cp in s_copies(s, first):
+                cp.start()
     for s in range(2):
         for i in range(NB):
             R[s, 0, pl.ds(EX * i, 8), :] = jnp.zeros((8, LANES), F32)
@@ -341,17 +341,9 @@
             FX[s, i + 1, :, :] = 0.5 * (c_own + R[s, 0, pl.ds(at + EX + 8, NB), :])
             FY[s, i, 0:NB, :] = 0.5 * (c_own + R[s, 0, pl.ds(at + 7, NB), :])
 
-    @pl.loop(0, 57)
-    def _(i):
-        for s in range(2):
-            for h in range(2):
-                R[s, h, pl.ds(pl.multiple_of(EX * i, 8), EX), :] = jnp.zeros((EX, LANES), F32)
-
-    when_all(has_side, lambda d: c_recv(d).wait_recv())
     for s in range(2):
         for d in range(4):
-            own = ces[d, s]
-            face = jnp.where(has_side[d], 0.5 * (own + cer[d, s]), own)
+            face = jnp.where(has_side[d], 0.0, ces[d, s])
             if d == 0:
                 FX[s, 0, :, :] = face
             elif d == 1:
@@ -360,11 +352,22 @@
                 FY[s, :, 0, :] = face
             else:
                 FY[s, :, NB, :] = face
-            FE[s, d] = face
+
+    @pl.loop(0, 57)
+    def _(i):
+        for s in range(2):
+            for h in range(2):
+                R[s, h, pl.ds(pl.multiple_of(EX * i, 8), EX), :] = jnp.zeros((EX, LANES), F32)
+
     for s in range(2):
         for h in range(2):
             f_copy(s, h).wait()
         stencil(s, None, True)
+    when_all(has_side, lambda d: c_recv(d).wait_recv())
+    for s in range(2):
+        for d in range(4):
+            FE[s, d] = jnp.where(has_side[d], 0.5 * (ces[d, s] + cer[d, s]), 0.0)
+    for s in range(2):
         wait_z(s, ROWS + COLS)
         edge_fix(s, 1.0, ROWS + COLS)
         send_early(s, 0, False)
@@ -427,11 +430,6 @@
         for h in range(2):
             U[s, h, pl.ds(m * g, g)] = U[s, h, pl.ds(m * g, g)] + om_ref[s] * z[h]
 
-    def write_out(s):
-        for h in range(2):
-            for m in range(CHUNKS):
-                o_copy(s, h, m).start()
-
     early(1, last)
     wait_frames(0, last)
     scatter_frames(0, last)
@@ -440,23 +438,29 @@
         finish(0, m)
         if m == LATE_AT:
             late(1, last)
-    write_out(0)
     inner_product(1)
     wait_frames(1, last)
     scatter_frames(1, last)
     fill_frame(1)
     for m in range(CHUNKS):
         finish(1, m)
-    write_out(1)
     when_all(has_side, lambda d: c_send(d).wait_send())
     for s in range(2):
         when_all(has_side, lambda d: z_send(s, d).wait_send())
         when_all(has_side, lambda d: e_copy(s, d, OPP_SIDE[d], last).wait_send(), COLS)
         when_all(has_side, lambda d: f_copy_remote(s, d, OPP_SIDE[d], last).wait_send())
         when_all(has_corner, lambda q: k_copy(s, q, 3 - q, last).wait_send())
-        for h in range(2):
-            for m in range(CHUNKS):
-                o_copy(s, h, m).wait()
+
+
+def write_out(u_ref, out_hbm, sem):
+    def copy(s, h, m):
+        g = NB // CHUNKS
+        return pltpu.make_async_copy(u_ref.at[s, h, pl.ds(m * g, g)], out_hbm.at[s, pl.ds(m * g, g), :, pl.ds(h * LANES, LANES)], sem.at[s, h, m])
+    for act in ("start", "wait"):
+        for s in range(2):
+            for h in range(2):
+                for m in range(CHUNKS):
+                    getattr(copy(s, h, m), act)()
 
 
 def solution(mesh):
@@ -467,20 +471,20 @@
         s_mat = jnp.swapaxes(solve_rows, 3, 4).reshape(num_sys, EX // 2, 7, 16, nb * nb)
         any_spec = pl.BlockSpec(memory_space=pl.ANY)
         dma = pltpu.SemaphoreType.DMA
-        return pl.pallas_call(
+        approx = pl.pallas_call(
             kernel,
             name="schwarz",
-            out_shape=jax.ShapeDtypeStruct(forcing.shape, F32),
-            in_specs=[any_spec, any_spec, pl.BlockSpec(memory_space=pltpu.VMEM), any_spec, pl.BlockSpec(memory_space=pltpu.SMEM)],
-            out_specs=any_spec,
+            out_shape=pltpu.VMEM((2, 2, NB, NB, LANES), F32),
+            in_specs=[any_spec, any_spec, any_spec, any_spec, pl.BlockSpec(memory_space=pltpu.SMEM)],
+            out_specs=pl.BlockSpec(memory_space=pltpu.VMEM),
             scratch_shapes=[
+                pltpu.VMEM((2, NB, NB), F32),
                 pltpu.VMEM((2, 24, 4, 16, NB * NB), BF16),
                 pltpu.VMEM((2, 4, 7, 16, NB * NB), BF16),
                 pltpu.VMEM((2, 24, 3, 16, NB * NB), BF16),
                 pltpu.VMEM((2, 2, 50, 64, LANES), F32),
                 pltpu.VMEM((2, 2, 57 * EX, LANES), F32),
                 pltpu.VMEM((2, EX * EX, 2 * LANES), BF16),
-                pltpu.VMEM((2, 2, NB, NB, LANES), F32),
                 pltpu.VMEM((2, NB + 1, NB, LANES), F32),
                 pltpu.VMEM((2, NB, EX, LANES), F32),
                 pltpu.VMEM((2, 4, NB, LANES), F32),
@@ -492,12 +496,22 @@
                 pltpu.VMEM((2, 2, 4, MG, NB, 2 * LANES), BF16),
                 pltpu.VMEM((2, 4, 32, 2 * LANES), BF16),
                 pltpu.VMEM((2, 2, 4, 32, 2 * LANES), BF16),
-                dma((2, 2)), dma((2, 2)), dma((2, 7)), dma((2, 2, CHUNKS)),
+                dma, dma((2, 2)), dma((2, 2)), dma((2, 7)),
                 dma((4,)), dma((4,)), dma((2, 4)), dma((2, 4)),
                 dma((2, 4)), dma((2, 2, 4)), dma((2, 4)), dma((2, 2, 4)), dma((2, 4)), dma((2, 2, 4)),
             ],
-            compiler_params=pltpu.CompilerParams(collective_id=0, has_side_effects=True, vmem_limit_bytes=66_000_000),
+            compiler_params=pltpu.CompilerParams(collective_id=0, has_side_effects=True, vmem_limit_bytes=61_500_000),
             cost_estimate=pl.CostEstimate(flops=30_000_000_000, bytes_accessed=43_000_000, transcendentals=0),
         )(forcing, init_guess, cell_coef, s_mat, relax_factor)
+        return pl.pallas_call(
+            write_out,
+            name="write_out",
+            out_shape=jax.ShapeDtypeStruct(forcing.shape, F32),
+            in_specs=[pl.BlockSpec(memory_space=pltpu.VMEM)],
+            out_specs=any_spec,
+            scratch_shapes=[dma((2, 2, CHUNKS))],
+            compiler_params=pltpu.CompilerParams(vmem_limit_bytes=8_000_000),
+            cost_estimate=pl.CostEstimate(flops=1_000_000, bytes_accessed=9_500_000, transcendentals=0),
+        )(approx)
 
     return jax.shard_map(local, mesh=mesh, in_specs=(grid_spec, grid_spec, P(None, "row", "col"), P(None, "row", "col", None, None), P(None)), out_specs=grid_spec, check_vma=False)

time: 84.8 us -> 78.7 us (0.928)
  local copies, waits for them, and re-layouts: 4.86 us -> 0 us
  Pallas kernels: 79.7 us -> 78.4 us
    unnamed x1 -> x0, local copies, waits for them, and re-layouts: 4.86 us -> none
    pallas_call x1 -> x2, Pallas kernels: 79.7 us -> 78.4 us  [the longest x1 76.2 us: local(): pl.pallas_call(kernel, name='schwarz', out_shape=pltpu.VMEM((2, 2, NB, NB...]
where the time goes in v3:
time: 78.7 us; the launch traced here: 78.6 us
  Pallas kernels  78.4 us (100%)
    pallas_call x1, Pallas kernels, local(): pl.pallas_call(kernel, name='schwarz', out_shape=pltpu.VMEM((2, 2, NB, NB...  76.2 us
    pallas_call x1, Pallas kernels, local(): pl.pallas_call(write_out, name='write_out', out_shape=jax.ShapeDtypeStruc...  2.27 us

profile of v3, /device:TPU:0, one launch (start us, length us, event | category | flops | bytes accessed | tf_op | source)
XLA Modules:
  0.0 78.6 jit_solution(3029077593434294729)
XLA Ops:
  0.0 76.2 %schwarz.1.u_ref = f32[2,2,48,48,128]{4,3,2,1,0:T(8,128)S(1)} custom-call(f32[2,48,48,256]{3,2,1,0:T(8,128)} %f_hbm.1, f32[2,48,48,256]{3,2,1,0:T(8,128)} %u_hbm.1, f32[2,48,48]{2,1,0:T(8,128)} %c_hbm.1, bf16[2,28,7,16,2304]{4,3,2,1,0:T(8,128)(2,1)} %bitcast.3, f32[2]{0:T(128)} %om_ref.1), custom_call_target="tpu_custom_call" | custom-call | flops 30000001024 | bytes 43000000 | tf_op jit(solution)/shard_map/schwarz/pallas_call | solution.py:474
  76.2 2.3 %write_out.1 = f32[2,48,48,256]{3,2,1,0:T(8,128)} custom-call(f32[2,2,48,48,128]{4,3,2,1,0:T(8,128)S(1)} %schwarz.1.u_ref), custom_call_target="tpu_custom_call" | custom-call | flops 1000000 | bytes 9500000 | tf_op jit(solution)/shard_map/write_out/pallas_call | solution.py:506

commit v4 on v3

--- a/solution.py
+++ b/solution.py
@@ -331,9 +331,6 @@
             for cp in s_copies(s, first):
                 cp.start()
     for s in range(2):
-        for i in range(NB):
-            R[s, 0, pl.ds(EX * i, 8), :] = jnp.zeros((8, LANES), F32)
-
         @pl.loop(0, NB)
         def _(i):
             at = pl.multiple_of(EX * i, 8)
@@ -353,12 +350,6 @@
             else:
                 FY[s, :, NB, :] = face
 
-    @pl.loop(0, 57)
-    def _(i):
-        for s in range(2):
-            for h in range(2):
-                R[s, h, pl.ds(pl.multiple_of(EX * i, 8), EX), :] = jnp.zeros((EX, LANES), F32)
-
     for s in range(2):
         for h in range(2):
             f_copy(s, h).wait()
@@ -431,14 +422,13 @@
             U[s, h, pl.ds(m * g, g)] = U[s, h, pl.ds(m * g, g)] + om_ref[s] * z[h]
 
     early(1, last)
+    inner_product(1)
+    late(1, last)
     wait_frames(0, last)
     scatter_frames(0, last)
     fill_frame(0)
     for m in range(CHUNKS):
         finish(0, m)
-        if m == LATE_AT:
-            late(1, last)
-    inner_product(1)
     wait_frames(1, last)
     scatter_frames(1, last)
     fill_frame(1)

time: 78.7 us -> 77.7 us (0.987)
  Pallas kernels: 78.4 us -> 77.4 us
    pallas_call x1, Pallas kernels: 76.2 us -> 75.2 us  [local(): pl.pallas_call(kernel, name='schwarz', out_shape=pltpu.VMEM((2, 2, NB, NB...]
where the time goes in v4:
time: 77.7 us; the launch traced here: 77.6 us
  Pallas kernels  77.4 us (100%)
    pallas_call x1, Pallas kernels, local(): pl.pallas_call(kernel, name='schwarz', out_shape=pltpu.VMEM((2, 2, NB, NB...  75.2 us
    pallas_call x1, Pallas kernels, local(): pl.pallas_call(write_out, name='write_out', out_shape=jax.ShapeDtypeStruc...  2.27 us

profile of v4, /device:TPU:0, one launch (start us, length us, event | category | flops | bytes accessed | tf_op | source)
XLA Modules:
  0.0 77.6 jit_solution(1132492887841352870)
XLA Ops:
  0.0 75.2 %schwarz.1.u_ref = f32[2,2,48,48,128]{4,3,2,1,0:T(8,128)S(1)} custom-call(f32[2,48,48,256]{3,2,1,0:T(8,128)} %f_hbm.1, f32[2,48,48,256]{3,2,1,0:T(8,128)} %u_hbm.1, f32[2,48,48]{2,1,0:T(8,128)} %c_hbm.1, bf16[2,28,7,16,2304]{4,3,2,1,0:T(8,128)(2,1)} %bitcast.3, f32[2]{0:T(128)} %om_ref.1), custom_call_target="tpu_custom_call" | custom-call | flops 30000001024 | bytes 43000000 | tf_op jit(solution)/shard_map/schwarz/pallas_call | solution.py:464
  75.2 2.3 %write_out.1 = f32[2,48,48,256]{3,2,1,0:T(8,128)} custom-call(f32[2,2,48,48,128]{4,3,2,1,0:T(8,128)S(1)} %schwarz.1.u_ref), custom_call_target="tpu_custom_call" | custom-call | flops 1000000 | bytes 9500000 | tf_op jit(solution)/shard_map/write_out/pallas_call | solution.py:496
